TPU v7x, 32 devices: a whole 2x2x4 slice. The times are simulated.
32 devices in a mesh: row: 8 (over z, x), col: 4 (over y, core).
Axes of the slice: x: 2, y: 2, z: 4, core: 2. Of those that a mesh axis runs over, the one named last changes fastest.
Arguments:
- coeffs: bfloat16 [1024, 128, 128], P(('row', 'col')), as said below
- tiles: int32 [1024, 1], replicated, may hold values from 0 to 7; in each aligned block of 32 rows (0 to 31, 32 to 63, ...) at most 5 rows name the same one
- primal: bfloat16 [1024, 1024], replicated, as said below
- dual_inverse: bfloat16 [1024, 1024], replicated, as said below
Outputs:
- schur: float32 [1024, 1024], P('row', 'col')
Inputs may be any that keep to these rules, and one draw needn't show every extreme that they name: `tiles`: within each aligned block of 32 constraints (the constraints of one device) no tile is named more than 5 times, a bound that some block reaches. Each coeffs[i] is symmetric. `primal`: Symmetric. `dual_inverse`: Symmetric.
All inputs are finite; a program needn't handle non-finite values.
Results may differ from a plain program's by a relative error of at most 0.0022.
Values may be sent and summed in bfloat16 or wider, within the bound.
A program may use at most 128 MiB of HBM per device.

v0:
```python
import jax
import jax.numpy as jnp
from jax import lax
from jax.sharding import PartitionSpec as P

MOST = 5


def slot_ranks(tile_group, first_tile, tile_width):
    labels = first_tile + jnp.arange(tile_width, dtype=jnp.int32)
    member = (tile_group[:, :, None] == labels[None, None, :]).astype(jnp.int32)
    before = jnp.cumsum(member, axis=1) - member
    return (member, jnp.sum(before * member, axis=2))


def slot_picks(tile_group, first_tile, tile_width, slot_depth):
    member, ordinal = slot_ranks(tile_group, first_tile, tile_width)
    levels = jnp.arange(slot_depth, dtype=jnp.int32)
    chosen = member[:, :, :, None] * (
        ordinal[:, :, None, None] == levels[None, None, None, :]
    ).astype(jnp.int32)
    return jnp.transpose(chosen, (0, 2, 3, 1)).astype(jnp.bfloat16)


def shards(coeffs, tiles, primal, dual_inverse):
    col_size = lax.axis_size("col")
    row_size = lax.axis_size("row")
    col_index = lax.axis_index("col")
    row_index = lax.axis_index("row")
    own_count = coeffs.shape[0]
    tile_size = coeffs.shape[1]
    tile_count = primal.shape[0] // tile_size
    per_col = tile_count // col_size
    slot_depth = MOST
    tile_area = tile_size * tile_size
    tile_ids = tiles[:, 0]
    row_count = col_size * own_count
    first_tile = col_index * per_col
    row_coeffs = lax.all_gather(coeffs, "col", axis=0, tiled=True)
    row_tiles = lax.dynamic_slice_in_dim(tile_ids, row_index * row_count, row_count)
    primal_strip = lax.dynamic_slice_in_dim(primal, first_tile * tile_size, per_col * tile_size, 1)
    primal_strip = primal_strip.reshape(tile_count, tile_size, per_col, tile_size)
    primal_pick = jnp.take(primal_strip, row_tiles, axis=0)
    product_tile = jnp.einsum(
        "iab,ibvc->ivac", row_coeffs, primal_pick, preferred_element_type=jnp.float32
    ).astype(jnp.bfloat16)
    dual_strip = lax.dynamic_slice_in_dim(
        dual_inverse, first_tile * tile_size, per_col * tile_size, 0
    )
    dual_strip = dual_strip.reshape(per_col, tile_size, tile_count, tile_size)
    dual_pick = jnp.take(dual_strip, row_tiles, axis=2)
    reduced = jnp.einsum(
        "ivba,vcib->ivac", product_tile, dual_pick, preferred_element_type=jnp.float32
    ).astype(jnp.bfloat16)
    reduced = reduced.reshape(row_count, per_col, tile_area)
    chosen_slots = slot_picks(
        row_tiles.reshape(col_size, own_count), first_tile, per_col, slot_depth
    )
    routed = jnp.einsum(
        "gvqk,gkx->gvqx",
        chosen_slots,
        row_coeffs.reshape(col_size, own_count, tile_area),
        preferred_element_type=jnp.float32,
    ).astype(jnp.bfloat16)
    values = jnp.einsum(
        "ivx,svqx->isvq",
        reduced,
        lax.all_gather(routed, "row", axis=0, tiled=True),
        preferred_element_type=jnp.float32,
    )
    home_span = row_size * per_col * slot_depth
    values = values.reshape(row_count, col_size, home_span)
    landed = lax.all_to_all(values, "col", split_axis=1, concat_axis=1, tiled=True)
    landed = landed.reshape(row_count, col_size * home_span)
    home_tiles = lax.dynamic_slice_in_dim(
        tile_ids, col_index * row_size * own_count, row_size * own_count
    )
    home_tiles = home_tiles.reshape(row_size, own_count)
    member, ordinal = slot_ranks(home_tiles, 0, tile_count)
    owner_col = home_tiles // per_col
    within = home_tiles - owner_col * per_col
    sender = jnp.arange(row_size, dtype=jnp.int32)[:, None]
    column_pick = (
        owner_col * home_span + sender * (per_col * slot_depth) + within * slot_depth + ordinal
    )
    return jnp.take(landed, column_pick.reshape(-1), axis=1)


def solution(mesh):
    return jax.shard_map(
        shards,
        mesh=mesh,
        in_specs=(P(("row", "col"), None, None), P(), P(), P()),
        out_specs=P("row", "col"),
        check_vma=False,
    )
```

profile of v0, /device:TPU:0, one launch (start us, length us, event | category | flops | bytes accessed | tf_op | source)
XLA Modules:
  0.0 243.5 jit_solution(329211813767962392)
XLA Ops:
  6.5 0.0 copy-start
  6.5 0.0 all-gather.3.cloned.1.call-start
  6.5 0.7 all-gather.3.cloned.1.call-update
  7.3 0.0 all-gather.5.cloned.1.call-start
  7.3 0.7 fusion.41
  8.0 0.1 eq.64
  8.1 0.1 compare_convert_fusion
  8.2 0.1 reduce_window_sum.23
  8.2 0.2 fusion.35
  8.5 0.1 compare_convert_fusion.1
  8.5 37.6 %all-gather.3.cloned.1.call-done = bf16[128,128,128]{2,1,0:T(8,128)(2,1)} async-done(((bf16[32,128,128]{2,1,0:T(8,128)(2,1)}), bf16[128,128,128]{2,1,0:T(8,128)(2,1)}) %all-gather.3.cloned.1.call-update) | async-done | bytes 4194320 | tf_op jit(solution)/shard_map/all_gather | solution.py:39
  46.1 7.3 %reshape.93 = bf16[4,32,16384,1]{2,1,0,3:T(8,128)(2,1)} reshape(bf16[128,128,128]{2,1,0:T(8,128)(2,1)} %all-gather.3.cloned.1.call-done) | data formatting | bytes 8388608 | tf_op jit(solution)/shard_map/reshape | solution.py:62
  53.4 0.0 copy-start.1
  53.4 2.9 %convolution_convert_fusion = bf16[4,2,5,16384]{3,2,1,0:T(8,128)(2,1)S(1)} fusion(bf16[4,32,16384,1]{2,1,0,3:T(8,128)(2,1)} %reshape.93, s32[4,5,32]{2,1,0:T(8,128)S(1)} %fusion.39, s32[4,2,32]{2,1,0:T(2,128)S(1)} %compare_convert_fusion.1), kind=kOutput, calls=%fused_computation.3 | convolution fusion | flops 42600960 | bytes 5508608 | tf_op jit(solution)/shard_map/gvqk,gkx->gvqx/dot_general | solution.py:59
  56.3 2.6 %copy.45 = bf16[4,2,5,16384]{3,1,2,0:T(2,128)(2,1)} copy(bf16[4,2,5,16384]{3,2,1,0:T(8,128)(2,1)S(1)} %convolution_convert_fusion) | data formatting | bytes 2621440 | tf_op jit(solution)/shard_map/convert_element_type | solution.py:64
  58.9 0.0 all-gather.5.cloned.1.call-update
  58.9 0.0 copy-done
  58.9 0.1 constant_dynamic-slice_fusion
  59.0 0.1 reshape.97
  59.2 0.1 copy.47
  59.3 1.1 dynamic-slice_bitcast_fusion
  60.3 0.1 copy.62
  60.4 0.1 copy.49
  60.5 0.0 copy-done.1
  60.6 6.6 %gather_fusion = bf16[128,128,2,128]{3,1,2,0:T(8,128)(2,1)} fusion(bf16[8,128,2,128]{3,1,2,0:T(8,128)(2,1)S(1)} %copy.47, s32[1024]{0:T(1024)S(1)} %pad_clamp_fusion.1), kind=kCustom, calls=%fused_computation | custom fusion | bytes 16777728 | tf_op jit(solution)/shard_map/jit(_take)/gather | solution.py:43
  67.2 6.6 %gather_fusion.1 = bf16[128,2,128,128]{3,2,1,0:T(8,128)(2,1)} fusion(bf16[2,128,8,128]{3,1,2,0:T(8,128)(2,1)S(1)} %copy.49, s32[1024]{0:T(1024)S(1)} %pad_clamp_fusion.1), kind=kCustom, calls=%fused_computation.1 | custom fusion | bytes 16777728 | tf_op jit(solution)/shard_map/jit(_take)/gather | solution.py:51
  73.9 0.1 eq.60
  74.0 0.1 copy.43
  74.1 0.7 fusion.44
  74.8 0.1 copy.44
  74.9 0.1 reduce_sum.21
  74.9 0.1 add.72
  75.0 0.1 add.73
  75.1 15.0 %fusion.11 = bf16[128,2,128,128]{3,2,1,0:T(8,128)(2,1)} fusion(bf16[128,2,128,128]{3,2,1,0:T(8,128)(2,1)} %gather_fusion.1, pred[128]{0:T(512)(128)(4,1)S(1)} %get-tuple-element.7, bf16[128,128,2,128]{3,1,2,0:T(8,128)(2,1)} %gather_fusion, bf16[128,128,128]{2,1,0:T(8,128)(2,1)} %all-gather.3.cloned.1.call-done), kind=kOutput, calls=%fused_computation.15 | convolution fusion | flops 2164260864 | bytes 29360256 | tf_op jit(solution)/shard_map/ivba,vcib->ivac/dot_general | solution.py:52
  90.1 12.6 %reshape.66 = bf16[128,2,16384]{2,1,0:T(2,128)(2,1)} reshape(bf16[128,2,128,128]{3,2,1,0:T(8,128)(2,1)} %fusion.11) | data formatting | bytes 16777216 | tf_op jit(solution)/shard_map/reshape | solution.py:55
  102.6 106.9 %all-gather.5.cloned.1.call-done = bf16[32,2,5,16384]{3,1,2,0:T(2,128)(2,1)} async-done(((bf16[4,2,5,16384]{3,1,2,0:T(2,128)(2,1)}), bf16[32,2,5,16384]{3,1,2,0:T(2,128)(2,1)}) %all-gather.5.cloned.1.call-update) | async-done | bytes 10485776 | tf_op jit(solution)/shard_map/all_gather | solution.py:68
  209.6 16.4 %fusion.28 = f32[128,32,2,5]{0,1,3,2:T(8,128)S(1)} fusion(bf16[128,2,16384,1]{2,1,0,3:T(2,128)(2,1)} %bitcast.36, bf16[32,2,5,16384]{3,1,2,0:T(2,128)(2,1)} %all-gather.5.cloned.1.call-done), kind=kOutput, calls=%fused_computation.20 | convolution fusion | flops 1342177280 | bytes 19038208 | tf_op jit(solution)/shard_map/ivx,svqx->isvq/dot_general | solution.py:65
  226.0 0.1 copy.52
  226.1 0.7 reshape.67
  226.8 3.3 %all-to-all-start = ((f32[128,4,80]{0,2,1:T(8,128)}), f32[128,4,80]{0,2,1:T(8,128)S(1)}, u32[]{:S(2)}, u32[]{:S(2)}) async-start(f32[128,4,80]{0,2,1:T(8,128)} %reshape.67), calls=%async_computation | async-start | bytes 327680 | tf_op jit(solution)/shard_map/all_to_all | solution.py:73
  230.2 4.9 %all-to-all-done = f32[128,4,80]{0,2,1:T(8,128)S(1)} async-done(((f32[128,4,80]{0,2,1:T(8,128)}), f32[128,4,80]{0,2,1:T(8,128)S(1)}, u32[]{:S(2)}, u32[]{:S(2)}) %all-to-all-start) | async-done | bytes 163872 | tf_op jit(solution)/shard_map/all_to_all | solution.py:73
  235.0 0.7 gather_fusion.2
  235.8 0.1 select_bitcast_fusion
  235.9 0.8 copy.53
  (8 shorter events, 0.1 us)
Async XLA Ops:
  6.5 52.4 %copy-start = (bf16[1024,1024]{1,0:T(8,128)(2,1)S(1)}, bf16[1024,1024]{1,0:T(8,128)(2,1)}, u32[]{:S(2)}) copy-start(bf16[1024,1024]{1,0:T(8,128)(2,1)} %param.6) | copy-start | bytes 6291460
  6.5 39.6 %all-gather.3.cloned.1.call-start = ((), (), s32[]{:S(2)}) async-start(), calls=%async_computation.1 | async-start | bytes 5242880 | tf_op jit(solution)/shard_map/all_gather | solution.py:39
  7.3 202.3 %all-gather.5.cloned.1.call-start = ((), (), s32[]{:S(2)}) async-start(), calls=%async_computation.2 | async-start | bytes 11796480 | tf_op jit(solution)/shard_map/all_gather | solution.py:68
  53.4 7.1 %copy-start.1 = (s32[1024,1]{0,1:T(1,128)S(1)}, s32[1024,1]{0,1:T(1,128)}, u32[]{:S(2)}) copy-start(s32[1024,1]{0,1:T(1,128)} %param.5) | copy-start | bytes 12292
  226.8 8.3 %all-to-all-start = ((f32[128,4,80]{0,2,1:T(8,128)}), f32[128,4,80]{0,2,1:T(8,128)S(1)}, u32[]{:S(2)}, u32[]{:S(2)}) async-start(f32[128,4,80]{0,2,1:T(8,128)} %reshape.67), calls=%async_computation | async-start | bytes 327680 | tf_op jit(solution)/shard_map/all_to_all | solution.py:73
Sparse Core Ops, SparseCore 0:
  8.9 37.1 all-gather.2
  59.0 150.4 all-gather.4
where the time goes:
time: 244 us; the launch traced here: 243 us
  waiting for transfers between devices  150 us (61%)
  local copies, waits for them, and re-layouts  40.8 us (17%)
  matrix products  34.3 us (14%)
  between operations  13.5 us (6%)
  starting transfers between devices  3.39 us (1%)
    all_gather x1, waiting for transfers between devices, shards(): lax.all_gather(routed, 'row', axis=0, tiled=True)  107 us
    all_gather x1, waiting for transfers between devices, shards(): row_coeffs = lax.all_gather(coeffs, 'col', axis=0, tiled=True)  37.6 us
    dot_general x1, matrix products, shards(): jnp.einsum('ivx,svqx->isvq', reduced, lax.all_gather(routed, 'row', axis=...  16.4 us
    dot_general x1, matrix products, shards(): jnp.einsum('ivba,vcib->ivac', product_tile, dual_pick, preferred_element_...  15 us
    reshape x1, local copies, waits for them, and re-layouts, shards(): reduced = reduced.reshape(row_count, per_col, tile_area)  12.6 us
    reshape x1, local copies, waits for them, and re-layouts, shards(): row_coeffs.reshape(col_size, own_count, tile_area)  7.31 us
    gather x1, local copies, waits for them, and re-layouts, shards(): dual_pick = jnp.take(dual_strip, row_tiles, axis=2)  6.64 us
    gather x1, local copies, waits for them, and re-layouts, shards(): primal_pick = jnp.take(primal_strip, row_tiles, axis=0)  6.64 us
  transfers between devices with their start and end apart: 3, of which 3 were waited for; matrix products, arithmetic and copies ran while one was open for 18% of the time, Pallas kernels for 0%

commit v1 on v0

v1 whole, which is shorter than its diff:
```python
import functools

import jax
import jax.numpy as jnp
from jax import lax
from jax.experimental import pallas as pl
from jax.experimental.pallas import tpu as pltpu
from jax.sharding import PartitionSpec as P

MOST = 5
CORES = 2
STEP = 4
GROUP = 16
MESH = pl.DeviceIdType.MESH


def slot_ranks(tile_group, first_tile, tile_width):
    labels = first_tile + jnp.arange(tile_width, dtype=jnp.int32)
    member = (tile_group[:, :, None] == labels[None, None, :]).astype(jnp.int32)
    before = jnp.cumsum(member, axis=1) - member
    return (member, jnp.sum(before * member, axis=2))


def fast_size(row_size):
    fast = 1
    while (2 * fast) * (2 * fast) <= row_size:
        fast *= 2
    return fast


def kernel(
    fast, tiles_ref, coeffs_ref, routed_ref, right_ref, left_ref,
    cols_ref, rows_ref, packed_ref,
    stage, col_recv, row_recv, local_sem, route_send, row_send, pass_send,
    up_send, down_send, plus_send, minus_send,
):
    row_size = lax.axis_size("row")
    col_size = lax.axis_size("col")
    slow = row_size // fast
    r = lax.axis_index("row")
    c = lax.axis_index("col")
    a = r // fast
    b = r % fast
    own = coeffs_ref.shape[0]
    size = coeffs_ref.shape[1]
    half = size // 2
    width = right_ref.shape[1]
    y_size = col_size // CORES
    y = c // CORES
    core = c % CORES

    def source(j):
        return ((y + j // CORES) % y_size) * CORES + (core + j % CORES) % CORES

    partner = y * CORES + (core + 1) % CORES

    barrier = pltpu.get_barrier_semaphore()
    for j in range(1, col_size):
        pl.semaphore_signal(barrier, inc=1, device_id=(r, source(j)), device_id_type=MESH)
    has_up, has_down = a < slow - 1, a > 0
    has_plus, has_minus = b < fast - 1, b > 0
    moves = [(has_up, r + fast), (has_down, r - fast), (has_plus, r + 1), (has_minus, r - 1)]
    for exists, there in moves:
        @pl.when(exists)
        def _():
            pl.semaphore_signal(barrier, inc=1, device_id=(there, c), device_id_type=MESH)
    near = sum(exists.astype(jnp.int32) for exists, _ in moves)
    pl.semaphore_wait(barrier, near + (col_size - 1))

    def remote(src, dst, send, recv, there):
        return pltpu.make_async_remote_copy(
            src_ref=src, dst_ref=dst, send_sem=send, recv_sem=recv,
            device_id=there, device_id_type=MESH,
        )

    finish = []

    routes = []
    for j in range(1, col_size):
        target = source(j)
        copy = remote(
            routed_ref.at[target], cols_ref.at[r, c], route_send.at[j],
            col_recv.at[r, c], (r, target),
        )
        copy.start()
        finish.append((None, copy))
    keep_cols = pltpu.make_async_copy(routed_ref.at[c], cols_ref.at[r, c], local_sem.at[0])
    keep_cols.start()
    keep_rows = pltpu.make_async_copy(coeffs_ref, rows_ref.at[c], local_sem.at[1])
    keep_rows.start()
    for j in range(1, col_size):
        if j == 1 or j % CORES == 0:
            copy = remote(
                coeffs_ref, rows_ref.at[c], row_send.at[j], row_recv.at[c], (r, source(j))
            )
            copy.start()
            finish.append((None, copy))

    def piece_wait(there_r, there_c):
        remote(
            cols_ref.at[there_r, there_c], cols_ref.at[there_r, there_c],
            local_sem.at[2], col_recv.at[there_r, there_c], (r, partner),
        ).wait_recv()

    def piece_send(valid, exists, there, pr, pc, send):
        copy = remote(
            cols_ref.at[pr, pc], cols_ref.at[pr, pc], send, col_recv.at[pr, pc], (there, c)
        )
        cond = exists if valid is None else jnp.logical_and(valid, exists)

        @pl.when(cond)
        def _():
            copy.start()

        finish.append((cond, copy))

    def handle(d, sign, j):
        pr = r - sign * d * fast
        pc = source(j)
        if d == 0:
            valid = None
            if j == 0:
                keep_cols.wait()
            else:
                piece_wait(pr, pc)
        else:
            valid = (a - d >= 0) if sign > 0 else (a + d < slow)

            @pl.when(valid)
            def _():
                piece_wait(pr, pc)
        k = (d if sign > 0 else d + slow - 1) * col_size + j
        if d == 0 or sign > 0:
            if d < slow - 1:
                piece_send(valid, has_up, r + fast, pr, pc, up_send.at[d * col_size + j])
        if d == 0 or sign < 0:
            if d < slow - 1:
                piece_send(valid, has_down, r - fast, pr, pc, down_send.at[d * col_size + j])
        piece_send(valid, has_plus, r + 1, pr, pc, plus_send.at[k])
        piece_send(valid, has_minus, r - 1, pr, pc, minus_send.at[k])

    events = [functools.partial(handle, 0, 1, j) for j in range(col_size)]
    for d in range(1, slow):
        for j in range(col_size):
            events.append(functools.partial(handle, d, 1, j))
            events.append(functools.partial(handle, d, -1, j))

    def cross(e, sign, ap, j):
        pr = ap * fast + b - sign * e
        pc = source(j)
        valid = (b - e >= 0) if sign > 0 else (b + e < fast)

        @pl.when(valid)
        def _():
            piece_wait(pr, pc)
        k = (2 * slow - 1) * col_size + ((e - 1) * slow + ap) * col_size + j
        if e < fast - 1:
            if sign > 0:
                piece_send(valid, has_plus, r + 1, pr, pc, plus_send.at[k])
            else:
                piece_send(valid, has_minus, r - 1, pr, pc, minus_send.at[k])

    crossings = []
    for e in range(1, fast):
        for ap in range(slow):
            for j in range(col_size):
                crossings.append(functools.partial(cross, e, 1, ap, j))
                crossings.append(functools.partial(cross, e, -1, ap, j))

    line = lax.broadcasted_iota(jnp.int32, (half, size), 0)
    lane = lax.broadcasted_iota(jnp.int32, (half, size), 1)
    left = lane < half
    below = jnp.logical_or(left, lane - half <= line)
    scale = jnp.where(lane - half == line, 0.5, 1.0).astype(jnp.float32)
    corner = jnp.where(lane == line, 0.5, 0.0).astype(jnp.float32)
    pitch = half + 8

    def row_step(pc, first):
        def body(n, carry):
            i = first + n
            t = tiles_ref[(r * col_size + pc) * own + i]
            block = rows_ref[pc, i]
            slot = lax.rem(i, GROUP)
            for u in range(width):
                w = jnp.dot(block, right_ref[t, u], preferred_element_type=jnp.float32)
                w = w.astype(jnp.bfloat16)
                w = jnp.concatenate([w[:, size:], w[:, :size]], axis=0)
                total = jnp.dot(left_ref[t, u], w, preferred_element_type=jnp.float32)
                top, bottom = total[:half], total[half:]
                main = jnp.where(below, bottom, pltpu.roll(top, half, 1)) * scale
                base = pl.multiple_of(slot * pitch, 8)
                stage[u, pl.ds(base, half), :] = main
                diag = jnp.sum(top * corner, axis=0, keepdims=True)
                stage[u, pl.ds(base + half, 8), :] = jnp.broadcast_to(diag, (8, size))
            return carry

        lax.fori_loop(0, STEP, body, 0)

    def row_flush(pc, first):
        start = pl.multiple_of(pc * own + first, GROUP)
        for u in range(width):
            for k in range(half + 1):
                part = stage[u, pl.ds(k, GROUP, stride=pitch), :]
                packed_ref[u, k, pl.ds(start, GROUP), :] = part.astype(jnp.bfloat16)

    def rows_ready(j):
        pc = source(j)
        if j == 0:
            keep_rows.wait()
            return
        copy = remote(
            rows_ref.at[pc], rows_ref.at[pc], pass_send.at[j], row_recv.at[pc], (r, partner)
        )
        copy.wait_recv()
        if j % CORES == 0:
            copy.start()
            finish.append((None, copy))

    work = []
    for j in range(col_size):
        work.append(functools.partial(rows_ready, j))

        def group(n, j=j):
            first = n * GROUP
            for s in range(0, GROUP, STEP):
                row_step(source(j), first + s)
            row_flush(source(j), first)

        for n in range(own // GROUP):
            first = n * GROUP
            for s in range(0, GROUP, STEP):
                work.append(functools.partial(row_step, source(j), first + s))
            work.append(functools.partial(row_flush, source(j), first))

    done = 0
    for k, event in enumerate(events):
        event()
        upto = len(work) * max(0, k + 1 - col_size // 2) // (len(events) - col_size // 2)
        while done < upto:
            work[done]()
            done += 1
    for event in crossings:
        event()
    for cond, copy in finish:
        if cond is None:
            copy.wait_send()
        else:
            pl.when(cond)(copy.wait_send)


def gather_and_reduce(fast, tile_ids, coeffs, routed, right, left):
    row_size = lax.axis_size("row")
    col_size = lax.axis_size("col")
    own, size, _ = coeffs.shape
    width = right.shape[1]
    slow = row_size // fast
    crossed = ((2 * slow - 1) + (fast - 1) * slow) * col_size
    vmem = pl.BlockSpec(memory_space=pltpu.VMEM)
    dma = pltpu.SemaphoreType.DMA
    return pl.pallas_call(
        functools.partial(kernel, fast),
        out_shape=(
            jax.ShapeDtypeStruct((row_size, col_size) + routed.shape[1:], jnp.bfloat16),
            jax.ShapeDtypeStruct((col_size,) + coeffs.shape, jnp.bfloat16),
            jax.ShapeDtypeStruct((width, size // 2 + 1, col_size * own, size), jnp.bfloat16),
        ),
        in_specs=[pl.BlockSpec(memory_space=pltpu.SMEM)] + [vmem] * 4,
        out_specs=(vmem, vmem, vmem),
        scratch_shapes=[
            pltpu.VMEM((width, GROUP * (size // 2 + 8), size), jnp.float32),
            dma((row_size, col_size)),
            dma((col_size,)),
            dma((3,)),
            dma((col_size,)),
            dma((col_size,)),
            dma((col_size,)),
            dma((slow * col_size,)),
            dma((slow * col_size,)),
            dma((crossed,)),
            dma((crossed,)),
        ],
        compiler_params=pltpu.CompilerParams(
            collective_id=0, has_side_effects=True, vmem_limit_bytes=60 * 1024 * 1024
        ),
    )(tile_ids, coeffs, routed, right, left)


def shards(coeffs, tiles, primal, dual_inverse):
    col_size = lax.axis_size("col")
    row_size = lax.axis_size("row")
    col_index = lax.axis_index("col")
    row_index = lax.axis_index("row")
    own, size, _ = coeffs.shape
    half = size // 2
    tile_count = primal.shape[0] // size
    per_col = tile_count // col_size
    slots = per_col * MOST
    tile_ids = tiles[:, 0]
    row_count = col_size * own
    first_tile = col_index * per_col

    line = lax.broadcasted_iota(jnp.int32, (half, size), 0)
    lane = lax.broadcasted_iota(jnp.int32, (half, size), 1)
    below = jnp.logical_or(lane < half, lane - half <= line)
    shifted = jnp.concatenate([coeffs[:, :half, half:], coeffs[:, :half, :half]], axis=2)
    main = jnp.where(below, coeffs[:, half:, :], shifted)
    corner = (lane == line).astype(coeffs.dtype)
    diag = jnp.sum(coeffs[:, :half, :] * corner, axis=1)
    own_tiles = lax.dynamic_slice_in_dim(tile_ids, (row_index * col_size + col_index) * own, own)
    member, ordinal = slot_ranks(own_tiles[None], 0, tile_count)
    levels = jnp.arange(MOST, dtype=jnp.int32)
    chosen = member[0][:, :, None] * (ordinal[0][:, None, None] == levels).astype(jnp.int32)
    offsets = jnp.arange(own, dtype=jnp.int32)
    origin = jnp.sum(chosen * offsets[:, None, None], axis=0).reshape(-1)
    main = jnp.take(main, origin, axis=0).reshape(col_size, slots * half, size)
    diag = jnp.take(diag, origin, axis=0).reshape(col_size, slots, size)
    extra = -(-slots // 16) * 16
    diag = jnp.pad(diag, ((0, 0), (0, extra - slots), (0, 0)))
    fill = -(slots * half) % 16
    routed = jnp.concatenate([main, diag], axis=1)
    routed = jnp.pad(routed, ((0, 0), (0, fill), (0, 0)))

    def strip(matrix):
        part = lax.dynamic_slice_in_dim(matrix, first_tile * size, per_col * size, 0)
        part = part.reshape(per_col, size, tile_count, size)
        return jnp.transpose(part, (2, 0, 1, 3))

    def stripe(matrix):
        part = lax.dynamic_slice_in_dim(matrix, first_tile * size, per_col * size, 1)
        part = part.reshape(tile_count, size, per_col, size)
        return jnp.transpose(part, (0, 2, 1, 3))

    left = jnp.concatenate([strip(primal), strip(dual_inverse)], axis=3)
    right = jnp.concatenate([stripe(primal), stripe(dual_inverse)], axis=3)
    cols, _, packed = gather_and_reduce(
        fast_size(row_size), tile_ids, coeffs, routed, right, left
    )
    main = cols[:, :, : slots * half].reshape(
        row_size * col_size, per_col, MOST, half, size
    )
    diag = cols[:, :, slots * half : slots * (half + 1)].reshape(
        row_size * col_size, per_col, MOST, size
    )
    values = jnp.einsum(
        "vaib,gvqab->igvq", packed[:, :half], main, preferred_element_type=jnp.float32
    ) + jnp.einsum("vib,gvqb->igvq", packed[:, half], diag, preferred_element_type=jnp.float32)
    home_span = row_size * slots
    values = values.reshape(row_count, col_size, home_span)
    landed = lax.all_to_all(values, "col", split_axis=1, concat_axis=1, tiled=True)
    landed = landed.reshape(row_count, col_size * home_span)
    home_tiles = lax.dynamic_slice_in_dim(
        tile_ids, col_index * row_size * own, row_size * own
    )
    home_tiles = home_tiles.reshape(row_size, own)
    _, ordinal = slot_ranks(home_tiles, 0, tile_count)
    owner_col = home_tiles // per_col
    within = home_tiles - owner_col * per_col
    sender = jnp.arange(row_size, dtype=jnp.int32)[:, None]
    column_pick = owner_col * home_span + sender * slots + within * MOST + ordinal
    pick = column_pick.reshape(1, -1) == jnp.arange(col_size * home_span, dtype=jnp.int32)[:, None]
    return jnp.dot(landed, pick.astype(jnp.float32), precision=lax.Precision.HIGHEST)


def solution(mesh):
    return jax.shard_map(
        shards,
        mesh=mesh,
        in_specs=(P(("row", "col"), None, None), P(), P(), P()),
        out_specs=P("row", "col"),
        check_vma=False,
    )
```

time: 244 us -> 112 us (0.46)
  waiting for transfers between devices: 150 us -> 2.18 us
  Pallas kernels: 0 us -> 76.5 us
  matrix products: 34.3 us -> 6.34 us
  local copies, waits for them, and re-layouts: 40.8 us -> 16 us
  between operations: 13.5 us -> 0.21 us
  other arithmetic: 1.37 us -> 6.88 us
    all_gather x2 -> x0, waiting for transfers between devices: 145 us -> none  [the longest x1 107 us: shards(): lax.all_gather(routed, 'row', axis=0, tiled=True)]
    pallas_call x0 -> x1, Pallas kernels: none -> 76.5 us  [gather_and_reduce(): pl.pallas_call(functools.partial(kernel, fast), out_shape=(jax.ShapeDtype...]
    dot_general x3, matrix products: 34.3 us -> 6.34 us  [the longest x1 5.14 us: shards(): jnp.einsum('vaib,gvqab->igvq', packed[:, :half], main, preferred_element_...]
    reshape x5 -> x8, local copies, waits for them, and re-layouts: 20.2 us -> 1.84 us  [the longest x4 1.49 us: stripe(): part = part.reshape(tile_count, size, per_col, size)]
    gather x3, local copies, waits for them, and re-layouts: 14 us -> 1.3 us  [the longest x1 0.67 us: shards(): main = jnp.take(main, origin, axis=0).reshape(col_size, slots * half, size)]
    slice x0 -> x4, local copies, waits for them, and re-layouts: none -> 5.17 us  [the longest x1 3 us: shards(): cols[:, :, :slots * half]]
    dynamic_slice x3 -> x4, local copies, waits for them, and re-layouts: 0.77 us -> 4.74 us  [the longest x1 2.16 us: stripe(): lax.dynamic_slice_in_dim(matrix, first_tile * size, per_col * size, 1)]
    concatenate x0 -> x3, other arithmetic: none -> 3.15 us  [the longest x1 1.12 us: shards(): right = jnp.concatenate([stripe(primal), stripe(dual_inverse)], axis=3)]
  transfers between devices with their start and end apart: 3 -> 1, of which waited for: 3 -> 1; matrix products, arithmetic and copies ran while one was open for 18% -> 3% of each run, Pallas kernels for 0% -> 0%
where the time goes in v1:
time: 112 us
  Pallas kernels  76.5 us (68%)
  local copies, waits for them, and re-layouts  16 us (14%)
  other arithmetic  6.88 us (6%)
  matrix products  6.34 us (6%)
  starting transfers between devices  3.86 us (3%)
  waiting for transfers between devices  2.18 us (2%)
    pallas_call x1, Pallas kernels, gather_and_reduce(): pl.pallas_call(functools.partial(kernel, fast), out_shape=(jax.ShapeDtype...  76.5 us
    dot_general x1, matrix products, shards(): jnp.einsum('vaib,gvqab->igvq', packed[:, :half], main, preferred_element_...  5.14 us
    all_to_all x1, starting transfers between devices, shards(): lax.all_to_all(values, 'col', split_axis=1, concat_axis=1, tiled=True)  3.86 us
    slice x1, local copies, waits for them, and re-layouts, shards(): cols[:, :, :slots * half]  3 us
  transfers between devices with their start and end apart: 1, of which 1 were waited for; matrix products, arithmetic and copies ran while one was open for 3% of the time, Pallas kernels for 0%

profile of v1, /device:TPU:0, one launch (start us, length us, event | category | flops | bytes accessed | tf_op | source)
XLA Modules:
  0.0 112.0 jit_solution(1283327223577131132)
XLA Ops:
  0.0 0.7 fusion.24
  0.7 0.1 fusion.21
  0.8 0.1 reduce_window_sum.22
  0.9 0.2 select_reduce_fusion
  1.1 0.2 multiply_reduce_fusion.1
  1.3 0.1 copy.38
  1.3 0.1 reshape.286
  1.4 0.1 reshape.285
  1.5 0.0 copy-start
  1.5 2.2 %constant_dynamic-slice_fusion.1 = (bf16[1024,256]{1,0:T(8,128)(2,1)}, bf16[1024,256]{1,0:T(8,128)(2,1)S(1)}) fusion(bf16[1024,1024]{1,0:T(8,128)(2,1)} %param.7, s32[]{:T(128)S(6)} %select_n.58, bf16[1024,1024]{1,0:T(8,128)(2,1)} %param.6), kind=kLoop, calls=%fused_computation.55 | loop fusion | bytes 2097156 | tf_op jit(solution)/shard_map/dynamic_slice | solution.py:329
  3.7 1.3 %dynamic-slice_bitcast_fusion = (bf16[32,8,8,128]{3,1,2,0:T(8,128)(2,1)S(1)}, bf16[32,8,8,128]{3,1,2,0:T(8,128)(2,1)S(1)}) fusion(bf16[1024,1024]{1,0:T(8,128)(2,1)} %param.7, s32[]{:T(128)S(6)} %select_n.58, bf16[1024,1024]{1,0:T(8,128)(2,1)} %param.6), kind=kLoop, calls=%fused_computation.22 | loop fusion | bytes 2097156
  5.0 0.0 copy-done
  5.0 1.2 %fusion.27 = (bf16[32,64,64]{2,1,0:T(8,128)(2,1)}, bf16[32,64,64]{2,1,0:T(8,128)(2,1)}) fusion(bf16[32,128,128]{2,1,0:T(8,128)(2,1)S(1)} %copy-done), kind=kLoop, calls=%fused_computation.65 | loop fusion | bytes 1048576 | tf_op jit(solution)/shard_map/slice | solution.py:305
  6.2 0.1 broadcast_in_dim.35
  6.3 0.1 broadcast_in_dim.36
  6.4 1.7 %maximum_select_fusion = (bf16[32,64,128]{2,1,0:T(8,128)(2,1)S(1)}, bf16[32,128]{1,0:T(8,128)(2,1)S(1)}) fusion(bf16[32,64,64]{2,1,0:T(8,128)(2,1)} %get-tuple-element.14, bf16[32,64,64]{2,1,0:T(8,128)(2,1)} %get-tuple-element.13, bf16[32,128,128]{2,1,0:T(8,128)(2,1)S(1)} %copy-done, pred[64,128]{1,0:T(8,128)(4,1)S(1)} %get-tuple-element.15, ...), kind=kLoop, calls=%fused_computation.17 | loop fusion | flops 2617344 | bytes 2129920 | tf_op jit(solution)/shard_map/jit(_where)/select_n | solution.py:306
  8.1 0.7 gather_fusion
  8.8 0.6 gather_fusion.1
  9.4 0.1 broadcast_select_fusion
  9.5 1.2 %reshape.316 = bf16[8,128,2,128]{3,2,1,0:T(2,128)(2,1)S(1)} reshape(bf16[1024,256]{1,0:T(8,128)(2,1)} %get-tuple-element.19) | data formatting | bytes 1048576 | tf_op jit(solution)/shard_map/reshape | solution.py:330
  10.6 0.1 copy.68
  10.7 0.1 reshape.315
  10.9 0.1 copy.69
  11.0 0.1 copy.59
  11.1 0.1 copy.70
  11.2 0.1 copy.58
  11.3 0.1 copy.71
  11.4 0.7 bitcast_select_fusion
  12.1 0.9 fusion.12.routed_ref
  13.0 1.1 pad_maximum_fusion.right_ref
  14.1 1.1 pad_maximum_fusion.1.left_ref
  15.2 76.5 %shard_map.46 = (bf16[8,4,656,128]{3,2,1,0:T(8,128)(2,1)}, bf16[4,32,128,128]{3,2,1,0:T(8,128)(2,1)}, bf16[2,65,128,128]{3,2,1,0:T(8,128)(2,1)}) custom-call(s32[1024]{0:T(1024)} %bitcast.65, bf16[32,128,128]{2,1,0:T(8,128)(2,1)} %coeffs_ref.1, bf16[4,656,128]{2,1,0:T(8,128)(2,1)} %fusion.12.routed_ref, bf16[8,2,128,256]{3,2,1,0:T(8,128)(2,1)} %pad_maximum_fusion.right_ref, ...), custom_call_target="tpu_custom_call" | custom-call | tf_op jit(solution)/shard_map/pallas_call | solution.py:260
  91.8 0.0 copy-start.1
  91.8 3.0 %slice.28 = bf16[8,4,640,128]{3,2,1,0:T(8,128)(2,1)S(1)} slice(bf16[8,4,656,128]{3,2,1,0:T(8,128)(2,1)} %get-tuple-element.7), slice={[0:8], [0:4], [0:640], [0:128]} | slice | bytes 10485760 | tf_op jit(solution)/shard_map/slice | solution.py:338
  94.8 0.9 slice.30
  95.7 0.0 copy-done.1
  95.8 5.1 %fusion.6 = f32[2,32,5,128]{3,1,2,0:T(8,128)S(1)} fusion(bf16[2,65,128,128]{3,2,1,0:T(8,128)(2,1)S(1)} %copy-done.1, bf16[32,2,5,64,128]{4,3,2,1,0:T(8,128)(2,1)S(1)} %bitcast.55), kind=kOutput, calls=%fused_computation.10 | convolution fusion | flops 671088640 | bytes 9601024 | tf_op jit(solution)/shard_map/vaib,gvqab->igvq/dot_general | solution.py:344
  100.9 0.2 fusion.5
  101.1 0.1 copy.48
  101.2 0.7 reshape.293
  101.9 3.9 %all-to-all-start = ((f32[128,4,80]{0,2,1:T(8,128)}), f32[128,4,80]{0,2,1:T(8,128)S(1)}, u32[]{:S(2)}, u32[]{:S(2)}) async-start(f32[128,4,80]{0,2,1:T(8,128)} %reshape.293), calls=%async_computation | async-start | bytes 327680 | tf_op jit(solution)/shard_map/all_to_all | solution.py:349
  105.7 0.5 broadcast.203
  106.3 1.3 %fusion.26 = (s32[256]{0:T(256)S(1)}, s32[256,1]{0,1:T(1,128)S(1)}) fusion(s32[]{:T(128)} %broadcast.203, s32[1024,1]{0,1:T(1,128)} %param.5, s32[]{:T(128)S(6)} %select_n.58), kind=kLoop, calls=%fused_computation.64 | loop fusion | bytes 3080 | tf_op jit(solution)/shard_map/dynamic_slice | solution.py:351
  107.6 0.1 eq.98
  107.7 0.1 copy.49
  107.8 0.7 fusion.28
  108.5 0.1 copy.50
  108.6 0.1 reduce_sum.45
  108.6 0.1 add.90
  108.7 0.1 add.91
  108.8 2.2 %all-to-all-done = f32[128,4,80]{0,2,1:T(8,128)S(1)} async-done(((f32[128,4,80]{0,2,1:T(8,128)}), f32[128,4,80]{0,2,1:T(8,128)S(1)}, u32[]{:S(2)}, u32[]{:S(2)}) %all-to-all-start) | async-done | bytes 163872 | tf_op jit(solution)/shard_map/all_to_all | solution.py:349
  111.0 1.0 fusion.13
  (12 shorter events, 0.1 us)
Async XLA Ops:
  1.5 3.5 %copy-start = (bf16[32,128,128]{2,1,0:T(8,128)(2,1)S(1)}, bf16[32,128,128]{2,1,0:T(8,128)(2,1)}, u32[]{:S(2)}) copy-start(bf16[32,128,128]{2,1,0:T(8,128)(2,1)} %coeffs_ref.1) | copy-start | bytes 3145732
  91.8 4.0 %copy-start.1 = (bf16[2,65,128,128]{3,2,1,0:T(8,128)(2,1)S(1)}, bf16[2,65,128,128]{3,2,1,0:T(8,128)(2,1)}, u32[]{:S(2)}) copy-start(bf16[2,65,128,128]{3,2,1,0:T(8,128)(2,1)} %get-tuple-element.8) | copy-start | bytes 12779524
  101.9 9.1 %all-to-all-start = ((f32[128,4,80]{0,2,1:T(8,128)}), f32[128,4,80]{0,2,1:T(8,128)S(1)}, u32[]{:S(2)}, u32[]{:S(2)}) async-start(f32[128,4,80]{0,2,1:T(8,128)} %reshape.293), calls=%async_computation | async-start | bytes 327680 | tf_op jit(solution)/shard_map/all_to_all | solution.py:349
